TPU v7x, 64 devices: a 2x2x8 block of a 4x4x8 slice. The times are simulated.
64 devices in a mesh: layer: 4 (over x, y), tensor: 16 (over z, core).
Axes of the slice: x: 2, y: 2, z: 8, core: 2. Of those that a mesh axis runs over, the one named last changes fastest.
The devices are a block of a 4x4x8 slice.
Arguments:
- gradient: bfloat16 [2048, 6144], P('layer', 'tensor'), parts along dimension 0
- left_stat: float32 [2048, 512], P(('layer', 'tensor')), parts along dimension 0
- right_stat: float32 [24576, 6144], P(('layer', 'tensor')), parts along dimension 0
- left_root: bfloat16 [2048, 512], P(('layer', 'tensor')), parts along dimension 0
- right_root: bfloat16 [24576, 6144], P(('layer', 'tensor')), parts along dimension 0
Outputs:
- output 1: float32 [2048, 512], P(('layer', 'tensor')), parts along dimension 0
- output 2: float32 [24576, 6144], P(('layer', 'tensor')), parts along dimension 0
- output 3: float32 [2048, 6144], P('layer', 'tensor'), parts along dimension 0
There are 4 independent parts. A program takes and returns all parts, laid end to end along the dimension named above; each array names one.
All inputs are finite; a program needn't handle non-finite values.
Results may differ from a plain program's by a relative error of at most 0.001.
Values are sent between devices in bfloat16 or wider.
A program may use at most 768 MiB of HBM per device.

v0:
```python
import jax
import jax.numpy as jnp
from jax import lax
from jax.sharding import PartitionSpec as P

EMA_DECAY = 0.9


def solution(mesh):
    row_spec = P(("layer", "tensor"), None)
    col_spec = P("layer", "tensor")

    def local_step(grad_local, left_block, right_block, left_root_block, right_root_block):
        grad_full = lax.all_gather(grad_local, "tensor", axis=1, tiled=True)
        left_part = jnp.einsum("mc,kc->mk", grad_local, grad_local, preferred_element_type=jnp.float32)
        left_sum = lax.psum_scatter(left_part, "tensor", scatter_dimension=0, tiled=True)
        left_new = EMA_DECAY * left_block + (1.0 - EMA_DECAY) * left_sum
        right_prod = jnp.einsum("mc,mn->cn", grad_local, grad_full, preferred_element_type=jnp.float32)
        right_new = EMA_DECAY * right_block + (1.0 - EMA_DECAY) * right_prod
        precond = jnp.einsum("mn,cn->mc", grad_full, right_root_block, preferred_element_type=jnp.float32).astype(jnp.bfloat16)
        left_root_full = lax.all_gather(left_root_block, "tensor", axis=0, tiled=True)
        direction = jnp.dot(left_root_full, precond, preferred_element_type=jnp.float32)
        return left_new, right_new, direction

    return jax.shard_map(local_step, mesh=mesh, in_specs=(col_spec, row_spec, row_spec, row_spec, row_spec), out_specs=(row_spec, row_spec, col_spec), check_vma=False)
```

profile of v0, /device:TPU:21, one launch (start us, length us, event | category | flops | bytes accessed | tf_op | source)
XLA Modules:
  0.0 142.5 jit_solution(10385581971022088275)
XLA Ops:
  7.2 0.1 reduce-scatter.2.cloned.1.call-start
  7.2 2.6 %fusion = f32[512,512]{1,0:T(8,128)} fusion(bf16[512,384]{1,0:T(8,128)(2,1)} %param.5), kind=kOutput, calls=%fused_computation.4 | convolution fusion | flops 201326592 | bytes 1441792 | tf_op jit(solution)/shard_map/mc,kc->mk/dot_general | solution.py:15
  9.8 0.1 reduce-scatter.2.cloned.1.call-update
  9.9 0.1 all-gather.2.cloned.1.call-start
  10.0 0.7 all-gather.2.cloned.1.call-update
  10.7 24.3 %all_gather.7 = bf16[512,512]{1,0:T(8,128)(2,1)S(1)} all-gather(bf16[32,512]{1,0:T(8,128)(2,1)} %param.8), channel_id=1, replica_groups=mesh['layer'=4,'tensor'=16] {'tensor'}, dimensions={0}, use_global_device_ids=true | all-gather | bytes 557056 | tf_op jit(solution)/shard_map/all_gather | solution.py:21
  35.0 32.7 %reduce-scatter.2.cloned.1.call-done = f32[32,512]{1,0:T(8,128)} async-done(((f32[512,512]{1,0:T(8,128)}), f32[32,512]{1,0:T(8,128)}) %reduce-scatter.2.cloned.1.call-update) | async-done | bytes 65552 | tf_op jit(solution)/shard_map/reduce_scatter | solution.py:16
  67.6 1.5 %multiply_add_fusion.1 = f32[32,512]{1,0:T(8,128)} fusion(f32[32,512]{1,0:T(8,128)} %reduce-scatter.2.cloned.1.call-done, f32[32,512]{1,0:T(8,128)} %param.6), kind=kLoop, calls=%fused_computation.3 | loop fusion | flops 49152 | bytes 196608 | tf_op jit(solution)/shard_map/add | solution.py:17
  69.1 0.0 copy-start
  69.1 44.8 %all-gather.2.cloned.1.call-done = bf16[512,6144]{1,0:T(8,128)(2,1)} async-done(((bf16[512,384]{1,0:T(8,128)(2,1)}), bf16[512,6144]{1,0:T(8,128)(2,1)}) %all-gather.2.cloned.1.call-update) | async-done | bytes 6291472 | tf_op jit(solution)/shard_map/all_gather | solution.py:14
  113.9 7.9 %convolution_bitcast_fusion = f32[512,384]{0,1:T(8,128)S(1)} fusion(bf16[512,512]{1,0:T(8,128)(2,1)S(1)} %all_gather.7, bf16[512,6144]{1,0:T(8,128)(2,1)} %all-gather.2.cloned.1.call-done, bf16[384,6144]{1,0:T(8,128)(2,1)} %param.9), kind=kOutput, calls=%fused_computation.1 | convolution fusion | flops 2617442304 | bytes 12320768 | tf_op jit(solution)/shard_map/dot_general | solution.py:22
  121.9 1.1 copy.8
  123.0 0.0 copy-done
  123.0 12.7 %multiply_add_fusion = f32[384,6144]{1,0:T(8,128)} fusion(f32[384,6144]{1,0:T(8,128)} %param.7, bf16[512,384]{1,0:T(8,128)(2,1)S(1)} %copy-done, bf16[512,6144]{1,0:T(8,128)(2,1)} %all-gather.2.cloned.1.call-done), kind=kOutput, calls=%fused_computation | convolution fusion | flops 2422996992 | bytes 25559040 | tf_op jit(solution)/shard_map/mc,mn->cn/dot_general | solution.py:18
Async XLA Ops:
  7.2 60.4 %reduce-scatter.2.cloned.1.call-start = ((), (), s32[]{:S(2)}) async-start(), calls=%async_computation.1 | async-start | bytes 1114112 | tf_op jit(solution)/shard_map/reduce_scatter | solution.py:16
  9.9 104.1 %all-gather.2.cloned.1.call-start = ((), (), s32[]{:S(2)}) async-start(), calls=%async_computation.2 | async-start | bytes 6684672 | tf_op jit(solution)/shard_map/all_gather | solution.py:14
  69.1 53.9 %copy-start = (bf16[512,384]{1,0:T(8,128)(2,1)S(1)}, bf16[512,384]{1,0:T(8,128)(2,1)}, u32[]{:S(2)}) copy-start(bf16[512,384]{1,0:T(8,128)(2,1)} %param.5) | copy-start | bytes 1179652
Sparse Core Ops, SparseCore 0:
  10.9 56.6 reduce-scatter.1
  69.2 44.6 all-gather.1
where the time goes:
time: 143 us
  waiting for transfers between devices  78.3 us (55%)
  blocking collectives  24.3 us (17%)
  matrix products  23.2 us (16%)
  between operations  14.1 us (10%)
  other arithmetic  1.51 us (1%)
    all_gather x1, waiting for transfers between devices, local_step(): grad_full = lax.all_gather(grad_local, 'tensor', axis=1, tiled=True)  44.8 us
    reduce_scatter x1, waiting for transfers between devices, local_step(): lax.psum_scatter(left_part, 'tensor', scatter_dimension=0, tiled=True)  32.7 us
    all_gather x1, blocking collectives, local_step(): lax.all_gather(left_root_block, 'tensor', axis=0, tiled=True)  24.3 us
    dot_general x1, matrix products, local_step(): jnp.einsum('mc,mn->cn', grad_local, grad_full, preferred_element_type=jnp...  12.7 us
    dot_general x1, matrix products, local_step(): jnp.dot(left_root_full, precond, preferred_element_type=jnp.float32)  7.91 us
  transfers between devices with their start and end apart: 2, of which 2 were waited for; matrix products, arithmetic and copies ran while one was open for 1% of the time, Pallas kernels for 0%

commit v1 on v0

v1 whole, which is shorter than its diff:
```python
import functools

import jax
import jax.numpy as jnp
from jax import lax
from jax.experimental import pallas as pl
from jax.experimental.pallas import tpu as pltpu
from jax.sharding import PartitionSpec as P

EMA_DECAY = 0.9
CHUNKS = 4
LOADS = 4
NT = (((1,), (1,)), ((), ()))


def _dot(a, b):
    return jnp.dot(a, b, preferred_element_type=jnp.float32)


def _dot_nt(a, b):
    return lax.dot_general(a, b, NT, preferred_element_type=jnp.float32)


def _gather_kernel(
    chips,
    g_hbm, lr_hbm, l_hbm, r_hbm, rr_hbm,
    gall, lrall, rnew, rrv, xacc, lacc, lold, gt,
    load_sem, ring_send, ring_recv, sis_send, sis_recv,
    lring_send, lring_recv, lsis_send, lsis_recv,
):
    half = chips // 2
    full = half - 1
    me = lax.axis_index("tensor")
    z, core = me // 2, me % 2
    sister = {"tensor": 2 * z + (1 - core)}
    right = {"tensor": 2 * ((z + 1) % chips) + core}
    left = {"tensor": 2 * ((z + chips - 1) % chips) + core}
    towards = (right, left)
    block_rows, block_cols = g_hbm.shape
    lr_rows = lr_hbm.shape[0]
    piece = block_rows // CHUNKS
    n_full = full * CHUNKS
    n_events = n_full + CHUNKS // 2

    def chip_at(side, dist):
        return (z + chips - dist) % chips if side == 0 else (z + dist) % chips

    def piece_at(side, n):
        k = n % CHUNKS if side == 0 else (n + CHUNKS // 2) % CHUNKS
        slot = 2 * chip_at(side, n // CHUNKS) + core
        return gall.at[slot, pl.ds(pl.multiple_of(k * piece, piece), piece), :]

    def ring_copy(side, n):
        ref = piece_at(side, n)
        return pltpu.make_async_remote_copy(
            ref, ref, ring_send.at[side, n], ring_recv.at[side, n],
            device_id=towards[side], device_id_type=pl.DeviceIdType.MESH)

    def ring_arrival(side, e):
        ref = piece_at(side, e + CHUNKS)
        return pltpu.make_async_remote_copy(
            ref, ref, ring_send.at[side, e], ring_recv.at[side, e],
            device_id=towards[side], device_id_type=pl.DeviceIdType.MESH)

    def sister_copy(ref, n):
        return pltpu.make_async_remote_copy(
            ref, ref, sis_send.at[n], sis_recv.at[n],
            device_id=sister, device_id_type=pl.DeviceIdType.MESH)

    def lr_at(slot):
        return lrall.at[pl.ds(pl.multiple_of(slot * lr_rows, lr_rows), lr_rows), :]

    def lr_half_at(slot, side):
        rows = lr_rows // 2
        start = pl.multiple_of(slot * lr_rows + side * rows, rows)
        return lrall.at[pl.ds(start, rows), :]

    def lr_ring_copy(ref, side, n):
        return pltpu.make_async_remote_copy(
            ref, ref, lring_send.at[side, n], lring_recv.at[side, n],
            device_id=towards[side], device_id_type=pl.DeviceIdType.MESH)

    def lr_sister_copy(ref, n):
        return pltpu.make_async_remote_copy(
            ref, ref, lsis_send.at[n], lsis_recv.at[n],
            device_id=sister, device_id_type=pl.DeviceIdType.MESH)

    own = gall.at[me]
    own_load = pltpu.make_async_copy(g_hbm, own, load_sem.at[0])
    own_load.start()
    lr_load = pltpu.make_async_copy(lr_hbm, lr_at(me), load_sem.at[1])
    lr_load.start()

    barrier = pltpu.get_barrier_semaphore()
    for peer in (right, left, sister):
        pl.semaphore_signal(barrier, inc=1, device_id=peer, device_id_type=pl.DeviceIdType.MESH)
    pl.semaphore_wait(barrier, 3)

    lr_load.wait()
    for side in (0, 1):
        lr_ring_copy(lr_at(me), side, 0).start()
    own_load.wait()
    for n in range(CHUNKS):
        for side in (0, 1):
            ring_copy(side, n).start()
    lr_sister_copy(lr_at(me), 0).start()
    sister_copy(own, 0).start()

    loads = [pltpu.make_async_copy(l_hbm, lold, load_sem.at[2])]
    rows = r_hbm.shape[0] // LOADS
    for i in range(LOADS):
        part = pl.ds(i * rows, rows)
        loads.append(pltpu.make_async_copy(r_hbm.at[part, :], rnew.at[part, :], load_sem.at[3 + i]))
        loads.append(pltpu.make_async_copy(rr_hbm.at[part, :], rrv.at[part, :], load_sem.at[3 + LOADS + i]))
    for load in loads:
        load.start()

    gt[...] = gall[me].T
    xacc[...] = jnp.zeros_like(xacc)
    lacc[...] = jnp.zeros_like(lacc)
    for load in loads:
        load.wait()

    def event(e):
        dist = e // CHUNKS + 1
        k = e % CHUNKS

        @pl.when(k == 0)
        def _():
            for side in (0, 1):
                slot = 2 * chip_at(side, dist) + core

                @pl.when(dist < half)
                def _():
                    arrived = lr_ring_copy(lr_at(slot), side, dist - 1)
                    arrived.wait_recv()

                    @pl.when(dist < full)
                    def _():
                        lr_ring_copy(lr_at(slot), side, dist).start()

                    @pl.when(dist == full)
                    def _():
                        lr_ring_copy(lr_half_at(slot, side), side, full).start()

                    lr_sister_copy(lr_at(slot), 1 + side * full + dist - 1).start()

                @pl.when(dist == half)
                def _():
                    lr_ring_copy(lr_half_at(slot, side), side, full).wait_recv()
                    lr_sister_copy(lr_half_at(slot, side), 1 + 2 * full + side).start()

        for side in (0, 1):
            ring_arrival(side, e).wait_recv()

            @pl.when(e + CHUNKS < n_events)
            def _():
                ring_copy(side, e + CHUNKS).start()

            slot = 2 * chip_at(side, dist) + core

            @pl.when(dist < half)
            def _():
                @pl.when(k == CHUNKS - 1)
                def _():
                    sister_copy(gall.at[slot], 1 + side * full + dist - 1).start()

            @pl.when(dist == half)
            def _():
                sister_copy(
                    piece_at(side, e + CHUNKS),
                    1 + 2 * full + side * (CHUNKS // 2) + k).start()

    def accumulate(slot):
        cols = pl.ds(pl.multiple_of(slot * block_cols, block_cols), block_cols)
        g = gall[slot]
        rnew[:, cols] = EMA_DECAY * rnew[:, cols] + (1.0 - EMA_DECAY) * _dot(gt[...], g)
        xacc[...] += _dot_nt(g, rrv[:, cols])
        mine = gall[slot, pl.ds(pl.multiple_of(me * lr_rows, lr_rows), lr_rows), :]
        lacc[...] += _dot_nt(mine, g)

    def step(i, _):
        @pl.when(i != n_events - 1)
        def _():
            event(i - i // n_events)

        @pl.when(i < 2)
        def _():
            @pl.when(i == 1)
            def _():
                sister_copy(gall.at[2 * z + (1 - core)], 0).wait_recv()

            accumulate(2 * z + (core + i) % 2)

        @pl.when(i > 2)
        def _():
            q = i - 3
            dist = q // 4 + 1
            side = q % 2
            from_sister = (q % 4) // 2
            src = 2 * ((z + chips + (2 * side - 1) * dist) % chips) + (core + from_sister) % 2

            @pl.when(from_sister == 1)
            def _():
                sister_copy(gall.at[src], 1 + side * full + dist - 1).wait_recv()

            accumulate(src)

        return 0

    lax.fori_loop(0, n_events + 1, step, 0)

    far = chip_at(0, half)
    other = 2 * far + (1 - core)
    for side in (0, 1):
        for k in range(CHUNKS // 2):
            row = (k if side == 0 else k + CHUNKS // 2) * piece
            sister_copy(gall.at[other, pl.ds(row, piece), :],
                        1 + 2 * full + side * (CHUNKS // 2) + k).wait_recv()
        lr_sister_copy(lr_half_at(other, side), 1 + 2 * full + side).wait_recv()
        for dist in range(1, half):
            slot = 2 * chip_at(side, dist) + (1 - core)
            lr_sister_copy(lr_at(slot), 1 + side * full + dist - 1).wait_recv()
    lr_sister_copy(lr_at(2 * z + (1 - core)), 0).wait_recv()

    for side in (0, 1):
        for n in range(n_events):
            ring_copy(side, n).wait_send()
        for dist in range(half):
            slot = 2 * chip_at(side, dist) + core
            ref = lr_at(slot) if dist < full else lr_half_at(slot, side)
            lr_ring_copy(ref, side, dist).wait_send()
        for dist in range(1, half):
            slot = 2 * chip_at(side, dist) + core
            sister_copy(gall.at[slot], 1 + side * full + dist - 1).wait_send()
            lr_sister_copy(lr_at(slot), 1 + side * full + dist - 1).wait_send()
        for k in range(CHUNKS // 2):
            sister_copy(piece_at(side, n_full + CHUNKS + k),
                        1 + 2 * full + side * (CHUNKS // 2) + k).wait_send()
        lr_sister_copy(lr_half_at(2 * far + core, side), 1 + 2 * full + side).wait_send()
    sister_copy(own, 0).wait_send()
    lr_sister_copy(lr_at(me), 0).wait_send()


def _finish_kernel(
    chips,
    gall, lrall, rnew, rrv, xacc, lacc, lold, gt,
    l_out, r_out, d_out,
    rtail, dbuf, lbuf, sem,
):
    me = lax.axis_index("tensor")
    z = me // 2
    far = (z + chips // 2) % chips
    lr_rows = lold.shape[0]
    block_cols = gall.shape[2]
    width = 2 * block_cols

    def chip_cols(chip):
        return pl.ds(pl.multiple_of(chip * width, width), width)

    out = []
    for i in range(1, chips):
        cols = chip_cols((far + i) % chips)
        out.append(pltpu.make_async_copy(rnew.at[:, cols], r_out.at[:, cols], sem.at[i]))
        out[-1].start()

    x = xacc[...]
    left_sum = lacc[...]
    for c in (0, 1):
        slot = 2 * far + c
        cols = pl.ds(pl.multiple_of(slot * block_cols, block_cols), block_cols)
        g = gall[slot]
        x = x + _dot_nt(g, rrv[:, cols])
        mine = gall[slot, pl.ds(pl.multiple_of(me * lr_rows, lr_rows), lr_rows), :]
        left_sum = left_sum + _dot_nt(mine, g)
        rtail[:, c * block_cols:(c + 1) * block_cols] = (
            EMA_DECAY * rnew[:, cols] + (1.0 - EMA_DECAY) * _dot(gt[...], g))
    out.append(pltpu.make_async_copy(rtail, r_out.at[:, chip_cols(far)], sem.at[0]))
    out[-1].start()
    lbuf[...] = EMA_DECAY * lold[...] + (1.0 - EMA_DECAY) * left_sum
    out.append(pltpu.make_async_copy(lbuf, l_out, sem.at[chips]))
    out[-1].start()
    dbuf[...] = _dot(lrall[...], x.astype(jnp.bfloat16))
    out.append(pltpu.make_async_copy(dbuf, d_out, sem.at[chips + 1]))
    out[-1].start()
    for copy in out:
        copy.wait()


def solution(mesh):
    row_spec = P(("layer", "tensor"), None)
    col_spec = P("layer", "tensor")
    chips = mesh.shape["tensor"] // 2
    half = chips // 2
    full = half - 1
    n_events = full * CHUNKS + CHUNKS // 2

    def local_step(g, l, r, lr, rr):
        m, c = g.shape
        n = r.shape[1]
        f32, bf16 = jnp.float32, jnp.bfloat16
        dma = pltpu.SemaphoreType.DMA
        any_spec = pl.BlockSpec(memory_space=pl.ANY)
        vmem_spec = pl.BlockSpec(memory_space=pltpu.VMEM)
        held = (
            pltpu.VMEM((2 * chips, m, c), bf16),
            pltpu.VMEM((m, m), bf16),
            pltpu.VMEM(r.shape, f32),
            pltpu.VMEM(rr.shape, bf16),
            pltpu.VMEM((m, c), f32),
            pltpu.VMEM(l.shape, f32),
            pltpu.VMEM(l.shape, f32),
            pltpu.VMEM((c, m), bf16),
        )
        n_sis = 1 + 2 * full + CHUNKS
        n_lsis = 1 + 2 * full + 2
        state = pl.pallas_call(
            functools.partial(_gather_kernel, chips),
            out_shape=held,
            in_specs=[any_spec] * 5,
            out_specs=[vmem_spec] * len(held),
            scratch_shapes=[
                dma((3 + 2 * LOADS,)),
                dma((2, n_events)), dma((2, n_events)), dma((n_sis,)), dma((n_sis,)),
                dma((2, half)), dma((2, half)), dma((n_lsis,)), dma((n_lsis,)),
            ],
            compiler_params=pltpu.CompilerParams(
                collective_id=0, has_side_effects=True, vmem_limit_bytes=30 * 2**20),
        )(*(pltpu.with_memory_space_constraint(x, pltpu.HBM) for x in (g, lr, l, r, rr)))
        return pl.pallas_call(
            functools.partial(_finish_kernel, chips),
            out_shape=(
                jax.ShapeDtypeStruct(l.shape, f32),
                jax.ShapeDtypeStruct(r.shape, f32),
                jax.ShapeDtypeStruct((m, c), f32),
            ),
            in_specs=[vmem_spec] * len(held),
            out_specs=[any_spec] * 3,
            scratch_shapes=[
                pltpu.VMEM((r.shape[0], 2 * c), f32),
                pltpu.VMEM((m, c), f32),
                pltpu.VMEM(l.shape, f32),
                dma((chips + 2,)),
            ],
            compiler_params=pltpu.CompilerParams(vmem_limit_bytes=30 * 2**20),
        )(*state)

    return jax.shard_map(local_step, mesh=mesh, in_specs=(col_spec, row_spec, row_spec, row_spec, row_spec), out_specs=(row_spec, row_spec, col_spec), check_vma=False)
```

time: 143 us -> 50.6 us (0.35)
  waiting for transfers between devices: 78.3 us -> 0 us
  Pallas kernels: 0 us -> 49.9 us
  blocking collectives: 24.3 us -> 0 us
  matrix products: 23.2 us -> 0 us
  between operations: 14.1 us -> 0.64 us
  other arithmetic: 1.51 us -> 0 us
    pallas_call x0 -> x2, Pallas kernels: none -> 49.9 us  [the longest x1 44.6 us: local_step(): pl.pallas_call(functools.partial(_gather_kernel, chips), out_shape=held,...]
    all_gather x1 -> x0, waiting for transfers between devices: 44.8 us -> none  [local_step(): grad_full = lax.all_gather(grad_local, 'tensor', axis=1, tiled=True)]
    reduce_scatter x1 -> x0, waiting for transfers between devices: 32.7 us -> none  [local_step(): lax.psum_scatter(left_part, 'tensor', scatter_dimension=0, tiled=True)]
    all_gather x1 -> x0, blocking collectives: 24.3 us -> none  [local_step(): lax.all_gather(left_root_block, 'tensor', axis=0, tiled=True)]
    dot_general x3 -> x0, matrix products: 23.2 us -> none  [the longest x1 12.7 us: local_step(): jnp.einsum('mc,mn->cn', grad_local, grad_full, preferred_element_type=jnp...]
    add x1 -> x0, other arithmetic: 1.51 us -> none  [local_step(): left_new = EMA_DECAY * left_block + (1.0 - EMA_DECAY) * left_sum]
  transfers between devices with their start and end apart: 2 -> 0, of which waited for: 2 -> 0; matrix products, arithmetic and copies ran while one was open for 1% -> 0% of each run, Pallas kernels for 0% -> 0%
where the time goes in v1:
time: 50.6 us; the launch traced here: 50.5 us
  Pallas kernels  49.9 us (99%)
  between operations  0.64 us (1%)
    pallas_call x1, Pallas kernels, local_step(): pl.pallas_call(functools.partial(_gather_kernel, chips), out_shape=held,...  44.6 us
    pallas_call x1, Pallas kernels, local_step(): pl.pallas_call(functools.partial(_finish_kernel, chips), out_shape=(jax.S...  5.33 us

profile of v1, /device:TPU:21, one launch (start us, length us, event | category | flops | bytes accessed | tf_op | source)
XLA Modules:
  0.0 50.5 jit_solution(1409696864103755714)
XLA Ops:
  0.6 44.6 %shard_map.76 = (bf16[16,512,384]{2,1,0:T(8,128)(2,1)S(1)}, bf16[512,512]{1,0:T(8,128)(2,1)S(1)}, f32[384,6144]{1,0:T(8,128)S(1)}, bf16[384,6144]{1,0:T(8,128)(2...) custom-call(bf16[512,384]{1,0:T(8,128)(2,1)} %g_hbm.1, ...), custom_call_target="tpu_custom_call" | custom-call | tf_op jit(solution)/shard_map/pallas_call | solution.py:317
  45.2 5.3 %shard_map.77 = (f32[32,512]{1,0:T(8,128)}, f32[384,6144]{1,0:T(8,128)}, f32[512,384]{1,0:T(8,128)}) custom-call(bf16[16,512,384]{2,1,0:T(8,128)(2,1)S(1)} %get-tuple-element.11.gall, bf16[512,512]{1,0:T(8,128)(2,1)S(1)} %get-tuple-element.12.lrall, f32[384,6144]{1,0:T(8,128)S(1)} %get-tuple-element.13.rnew, bf16[384,6144]{1,0:T(8,128)(2,1)S(1)} %get-tuple-element.14.rrv, ...), custom_call_target="tpu_custom_call" | custom-call | tf_op jit(solution)/shard_map/pallas_call | solution.py:330
